TPU v7x, 32 devices: a whole 2x2x4 slice. The times are simulated.
32 devices in a mesh: row: 8 (over z, x), col: 4 (over y, core).
Axes of the slice: x: 2, y: 2, z: 4, core: 2. Of those that a mesh axis runs over, the one named last changes fastest.
Arguments:
- hidden_in: bfloat16 [32, 512, 1024], P('row', 'col'), may hold values from -6 to 6
- first_values: bfloat16 [32, 1024, 512], P('row', 'col'), may hold values from -6 to 6
- lengths: int32 [32, 4], P('row'), may hold values from 1 to 256, 512 in all within a row
- places: int32 [32, 512], P('row'), may hold values from 0 to 511, each once within a row
- gain_attn: float32 [1024], replicated, may hold values from 0.1 to 1.9
- gain_ffn: float32 [1024], replicated, may hold values from 0.1 to 1.9
- w_query: bfloat16 [1024, 1024], P('row', 'col'), may hold values from -0.1875 to 0.1875
- w_key: bfloat16 [1024, 1024], P('row', 'col'), may hold values from -0.1875 to 0.1875
- w_value: bfloat16 [1024, 1024], P('row', 'col'), may hold values from -0.1875 to 0.1875
- w_out: bfloat16 [1024, 1024], P('col', 'row'), may hold values from -3 to 3
- w_gate: bfloat16 [1024, 2816], P('row', 'col'), may hold values from -0.1875 to 0.1875
- w_up: bfloat16 [1024, 2816], P('row', 'col'), may hold values from -0.1875 to 0.1875
- w_down: bfloat16 [2816, 1024], P('col', 'row'), may hold values from -0.109375 to 0.109375
- out_grad: bfloat16 [32, 512, 1024], P('row', 'col'), may hold values from -6 to 6
Outputs:
- layer_out: bfloat16 [32, 512, 1024], P('row', 'col')
- grad_hidden: float32 [32, 512, 1024], P('row', 'col')
- grad_first_values: float32 [32, 1024, 512], P('row', 'col')
- grad_gain_attn: float32 [1024], replicated
- grad_gain_ffn: float32 [1024], replicated
- grad_w_query: float32 [1024, 1024], P('row', 'col')
- grad_w_key: float32 [1024, 1024], P('row', 'col')
- grad_w_value: float32 [1024, 1024], P('row', 'col')
- grad_w_out: float32 [1024, 1024], P('col', 'row')
- grad_w_gate: float32 [1024, 2816], P('row', 'col')
- grad_w_up: float32 [1024, 2816], P('row', 'col')
- grad_w_down: float32 [2816, 1024], P('col', 'row')
Inputs may be any that keep to these rules, and one draw needn't show every extreme that they name: Each row of lengths sums to 512; the largest length in the draw is 256. Each row of places holds every number of 0 to 511 once.
All inputs are finite; a program needn't handle non-finite values.
Results may differ from a plain program's by a relative error of at most 0.015.
Values may be sent and summed in bfloat16 or wider, within the bound.
A program may use at most 192 MiB of HBM per device.

v0:
```python
import jax
import jax.numpy as jnp
from jax import lax
from jax.sharding import PartitionSpec as P

D = 1024
HEAD_DIM = 64
TOK_MB = 512
MICRO = 4
EPSILON = 1e-06
MASKED = -1e30


def product(left, right):
    return jnp.dot(left, right, preferred_element_type=jnp.float32)


def product_left(left, right):
    return lax.dot_general(
        left, right, (((0,), (0,)), ((), ())), preferred_element_type=jnp.float32
    )


def product_right(left, right):
    return lax.dot_general(
        left, right, (((1,), (1,)), ((), ())), preferred_element_type=jnp.float32
    )


def token_places(lengths_row, count):
    ends_at = jnp.cumsum(lengths_row)
    index_row = jnp.arange(count, dtype=jnp.int32)
    segment_id = jnp.sum((index_row[:, None] >= ends_at[None, :]).astype(jnp.int32), axis=1)
    starts_at = ends_at - lengths_row
    one_hot = segment_id[:, None] == jnp.arange(lengths_row.shape[0], dtype=jnp.int32)[None, :]
    position = index_row - jnp.sum(jnp.where(one_hot, starts_at[None, :], 0), axis=1)
    return (segment_id, position)


def rotary_tables(position):
    half_dim = HEAD_DIM // 2
    freq_index = jnp.arange(half_dim, dtype=jnp.float32)
    inverse = 10000.0 ** (-freq_index / half_dim)
    angles = position.astype(jnp.float32)[:, None] * inverse[None, :]
    return (jnp.cos(angles)[:, None, :], jnp.sin(angles)[:, None, :])


def rotate(field, cosine, sine):
    half_dim = field.shape[-1] // 2
    first_half, second_half = (field[..., :half_dim], field[..., half_dim:])
    return jnp.concatenate(
        [first_half * cosine - second_half * sine, second_half * cosine + first_half * sine],
        axis=-1,
    )


def rotate_back(field, cosine, sine):
    half_dim = field.shape[-1] // 2
    first_half, second_half = (field[..., :half_dim], field[..., half_dim:])
    return jnp.concatenate(
        [first_half * cosine + second_half * sine, second_half * cosine - first_half * sine],
        axis=-1,
    )


def spread_tokens(values):
    return lax.all_gather(values, "col", axis=0, tiled=True)


def reduce_tokens(values):
    return lax.psum_scatter(values, "col", scatter_dimension=0, tiled=True)


def body(
    hidden_in,
    first_values,
    lengths,
    places,
    gain_attn,
    gain_ffn,
    w_query,
    w_key,
    w_value,
    w_out,
    w_gate,
    w_up,
    w_down,
    out_grad,
):
    width_col = w_query.shape[1]
    heads_col = width_col // HEAD_DIM
    block_rows = min(512, TOK_MB)
    block_count = TOK_MB // block_rows
    local_rows = hidden_in.shape[1]
    row_start = lax.axis_index("col") * local_rows
    score_scale = HEAD_DIM ** (-0.5)
    tiles = (w_query, w_key, w_value, w_out, w_gate, w_up, w_down)

    def own_rows(values):
        return lax.dynamic_slice_in_dim(values, row_start, local_rows)

    hidden_width = w_gate.shape[1]
    full_shapes = (
        (D, width_col),
        (D, width_col),
        (D, width_col),
        (width_col, D),
        (D, hidden_width),
        (D, hidden_width),
        (hidden_width, D),
    )
    grads_full = tuple((jnp.zeros(shape_item, jnp.float32) for shape_item in full_shapes))
    grads_tile = tuple((jnp.zeros(tile_item.shape, jnp.float32) for tile_item in tiles))
    gain_sum_one = jnp.zeros((D,), jnp.float32)
    gain_sum_two = jnp.zeros((D,), jnp.float32)
    out_pieces, input_pieces, value_pieces = ([], [], [])
    for micro_step in range(MICRO):
        gathered = (
            lax.all_gather(tiles[0], "row", axis=0, tiled=True),
            lax.all_gather(tiles[1], "row", axis=0, tiled=True),
            lax.all_gather(tiles[2], "row", axis=0, tiled=True),
            lax.all_gather(tiles[3], "row", axis=1, tiled=True),
            lax.all_gather(tiles[4], "row", axis=0, tiled=True),
            lax.all_gather(tiles[5], "row", axis=0, tiled=True),
            lax.all_gather(tiles[6], "row", axis=1, tiled=True),
        )
        wq_all, wk_all, wv_all, wo_all, wg_all, wu_all, wd_all = gathered
        places_mb = places[micro_step]
        packed_order = (
            jnp.zeros((TOK_MB,), jnp.int32).at[places_mb].set(jnp.arange(TOK_MB, dtype=jnp.int32))
        )
        stored_hidden, stored_grad = (
            lax.all_gather(hidden_in[micro_step], "col", axis=0, tiled=True),
            lax.all_gather(out_grad[micro_step], "col", axis=0, tiled=True),
        )
        hidden_full = jnp.take(stored_hidden, packed_order, axis=0).astype(jnp.float32)
        grad_full_rows = jnp.take(stored_grad, packed_order, axis=0)
        first_mb = jnp.take(jnp.transpose(first_values[micro_step]), packed_order, axis=0).astype(
            jnp.float32
        )
        hidden_mb = own_rows(hidden_full)
        grad_mb = own_rows(grad_full_rows)
        segment_id, position = token_places(lengths[micro_step], TOK_MB)
        cosine, sine = rotary_tables(position)
        token_index = jnp.arange(TOK_MB, dtype=jnp.int32)
        scale_full = lax.rsqrt(jnp.mean(hidden_full * hidden_full, axis=1, keepdims=True) + EPSILON)
        scale_one = own_rows(scale_full)
        normed_one = (hidden_full * scale_full * gain_attn).astype(jnp.bfloat16)
        query_raw = product(normed_one, wq_all).reshape(TOK_MB, heads_col, HEAD_DIM)
        key_raw = product(normed_one, wk_all).reshape(TOK_MB, heads_col, HEAD_DIM)
        queries = rotate(query_raw, cosine, sine).astype(jnp.bfloat16)
        keys = rotate(key_raw, cosine, sine).astype(jnp.bfloat16)
        values = (
            (0.5 * product(normed_one, wv_all) + 0.5 * first_mb)
            .astype(jnp.bfloat16)
            .reshape(TOK_MB, heads_col, HEAD_DIM)
        )

        def block_scores(start_row):
            query_index = start_row + jnp.arange(block_rows, dtype=jnp.int32)
            allowed = (segment_id[:, None] == segment_id[None, :]) & (
                query_index[:, None] >= token_index[None, :]
            )
            raw_scores = (
                jnp.einsum("qhd,khd->hqk", queries, keys, preferred_element_type=jnp.float32)
                * score_scale
            )
            return (queries, jnp.where(allowed[None], raw_scores, MASKED))

        def attend(block_index):
            query_block, scores = block_scores(block_index * block_rows)
            row_top = jnp.max(scores, axis=-1, keepdims=True)
            log_total = row_top + jnp.log(
                jnp.sum(jnp.exp(scores - row_top), axis=-1, keepdims=True)
            )
            probs = jnp.exp(scores - log_total).astype(jnp.bfloat16)
            mixed = jnp.einsum("hqk,khd->qhd", probs, values, preferred_element_type=jnp.float32)
            return (mixed.astype(jnp.bfloat16), log_total[..., 0])

        attended, log_totals = lax.map(attend, jnp.arange(block_count, dtype=jnp.int32))
        attended = attended.reshape(TOK_MB, width_col)
        mid_mb = hidden_mb + reduce_tokens(product(attended, wo_all))
        scale_two = lax.rsqrt(jnp.mean(mid_mb * mid_mb, axis=1, keepdims=True) + EPSILON)
        normed_two = spread_tokens((mid_mb * scale_two * gain_ffn).astype(jnp.bfloat16))
        gate_raw = product(normed_two, wg_all)
        up_raw = product(normed_two, wu_all)
        sigmoid_gate = jax.nn.sigmoid(gate_raw)
        silu_gate = gate_raw * sigmoid_gate
        hidden_act = (silu_gate * up_raw).astype(jnp.bfloat16)
        packed_out = (mid_mb + reduce_tokens(product(hidden_act, wd_all))).astype(jnp.bfloat16)
        grad_down = product_left(hidden_act, grad_full_rows)
        d_hidden = product_right(grad_full_rows, wd_all)
        d_gate = (
            d_hidden * up_raw * sigmoid_gate * (1.0 + gate_raw * (1.0 - sigmoid_gate))
        ).astype(jnp.bfloat16)
        d_up = (d_hidden * silu_gate).astype(jnp.bfloat16)
        grad_gate = product_left(normed_two, d_gate)
        grad_up = product_left(normed_two, d_up)
        d_normed_two = reduce_tokens(product_right(d_gate, wg_all) + product_right(d_up, wu_all))
        gain_sum_two = gain_sum_two + jnp.sum(d_normed_two * mid_mb * scale_two, axis=0)
        scaled_two = d_normed_two * gain_ffn
        stat_two = jnp.sum(scaled_two * mid_mb, axis=1, keepdims=True)
        d_mid = (
            grad_mb.astype(jnp.float32)
            + scale_two * scaled_two
            - mid_mb * (scale_two * scale_two * scale_two * stat_two / D)
        )
        d_branch = spread_tokens(d_mid.astype(jnp.bfloat16))
        grad_out = product_left(attended, d_branch)
        d_attended = (
            product_right(d_branch, wo_all)
            .astype(jnp.bfloat16)
            .reshape(TOK_MB, heads_col, HEAD_DIM)
        )

        def attend_back(carry, block_index):
            key_acc, value_acc = carry
            start_row = block_index * block_rows
            query_block, scores = block_scores(start_row)
            log_block = log_totals[block_index]
            probs = jnp.exp(scores - log_block[..., None])
            d_probs = jnp.einsum(
                "qhd,khd->hqk", d_attended, values, preferred_element_type=jnp.float32
            )
            inner_sum = jnp.sum(probs * d_probs, axis=-1, keepdims=True)
            d_scores = (probs * (d_probs - inner_sum)).astype(jnp.bfloat16)
            d_query = (
                jnp.einsum("hqk,khd->qhd", d_scores, keys, preferred_element_type=jnp.float32)
                * score_scale
            )
            key_acc = (
                key_acc
                + jnp.einsum(
                    "hqk,qhd->khd", d_scores, query_block, preferred_element_type=jnp.float32
                )
                * score_scale
            )
            value_acc = value_acc + jnp.einsum(
                "hqk,qhd->khd",
                probs.astype(jnp.bfloat16),
                d_attended,
                preferred_element_type=jnp.float32,
            )
            return ((key_acc, value_acc), d_query)

        empty_heads = jnp.zeros((TOK_MB, heads_col, HEAD_DIM), jnp.float32)
        (key_grads, value_grads), query_grads = lax.scan(
            attend_back, (empty_heads, empty_heads), jnp.arange(block_count, dtype=jnp.int32)
        )
        d_values = value_grads.astype(jnp.bfloat16).reshape(TOK_MB, width_col)
        half_values = 0.5 * d_values.astype(jnp.float32)
        value_pieces.append(jnp.transpose(jnp.take(half_values, places_mb, axis=0)))
        d_value_proj = half_values.astype(jnp.bfloat16)
        d_query_raw = (
            rotate_back(query_grads.reshape(TOK_MB, heads_col, HEAD_DIM), cosine, sine)
            .astype(jnp.bfloat16)
            .reshape(TOK_MB, width_col)
        )
        d_key_raw = (
            rotate_back(key_grads, cosine, sine).astype(jnp.bfloat16).reshape(TOK_MB, width_col)
        )
        grad_query = product_left(normed_one, d_query_raw)
        grad_key = product_left(normed_one, d_key_raw)
        grad_value = product_left(normed_one, d_value_proj)
        d_normed_one = reduce_tokens(
            product_right(d_query_raw, wq_all)
            + product_right(d_key_raw, wk_all)
            + product_right(d_value_proj, wv_all)
        )
        gain_sum_one = gain_sum_one + jnp.sum(d_normed_one * hidden_mb * scale_one, axis=0)
        scaled_one = d_normed_one * gain_attn
        stat_one = jnp.sum(scaled_one * hidden_mb, axis=1, keepdims=True)
        packed_input = (
            d_mid
            + scale_one * scaled_one
            - hidden_mb * (scale_one * scale_one * scale_one * stat_one / D)
        )
        out_whole, input_whole = (
            lax.all_gather(
                packed_out.astype(jnp.float32).astype(jnp.bfloat16), "col", axis=0, tiled=True
            ).astype(jnp.float32),
            lax.all_gather(packed_input.astype(jnp.bfloat16), "col", axis=0, tiled=True).astype(
                packed_input.dtype
            ),
        )
        stored_places = lax.dynamic_slice_in_dim(places_mb, row_start, local_rows)
        out_pieces.append(jnp.take(out_whole, stored_places, axis=0).astype(jnp.bfloat16))
        input_pieces.append(jnp.take(input_whole, stored_places, axis=0))
        new_grads = (grad_query, grad_key, grad_value, grad_out, grad_gate, grad_up, grad_down)
        grads_full = tuple((earlier + later for earlier, later in zip(grads_full, new_grads)))
    grads_tile = (
        lax.psum_scatter(
            grads_full[0].astype(jnp.bfloat16), "row", scatter_dimension=0, tiled=True
        ).astype(jnp.float32),
        lax.psum_scatter(
            grads_full[1].astype(jnp.bfloat16), "row", scatter_dimension=0, tiled=True
        ).astype(jnp.float32),
        lax.psum_scatter(
            grads_full[2].astype(jnp.bfloat16), "row", scatter_dimension=0, tiled=True
        ).astype(jnp.float32),
        lax.psum_scatter(
            grads_full[3].astype(jnp.bfloat16), "row", scatter_dimension=1, tiled=True
        ).astype(jnp.float32),
        lax.psum_scatter(
            grads_full[4].astype(jnp.bfloat16), "row", scatter_dimension=0, tiled=True
        ).astype(jnp.float32),
        lax.psum_scatter(
            grads_full[5].astype(jnp.bfloat16), "row", scatter_dimension=0, tiled=True
        ).astype(jnp.float32),
        lax.psum_scatter(
            grads_full[6].astype(jnp.bfloat16), "row", scatter_dimension=1, tiled=True
        ).astype(jnp.float32),
    )
    gain_grad_one, gain_grad_two = lax.psum((gain_sum_one, gain_sum_two), ("row", "col"))
    return (
        jnp.stack(out_pieces, axis=0),
        jnp.stack(input_pieces, axis=0),
        jnp.stack(value_pieces, axis=0),
        gain_grad_one,
        gain_grad_two,
        grads_tile[0],
        grads_tile[1],
        grads_tile[2],
        grads_tile[3],
        grads_tile[4],
        grads_tile[5],
        grads_tile[6],
    )


def solution(mesh):
    return jax.shard_map(
        body,
        mesh=mesh,
        in_specs=(
            P("row", "col", None),
            P("row", "col", None),
            P("row", None),
            P("row", None),
            P(),
            P(),
            P("row", "col"),
            P("row", "col"),
            P("row", "col"),
            P("col", "row"),
            P("row", "col"),
            P("row", "col"),
            P("col", "row"),
            P("row", "col", None),
        ),
        out_specs=(
            P("row", "col", None),
            P("row", "col", None),
            P("row", "col", None),
            P(),
            P(),
            P("row", "col"),
            P("row", "col"),
            P("row", "col"),
            P("col", "row"),
            P("row", "col"),
            P("row", "col"),
            P("col", "row"),
        ),
        check_vma=False,
    )
```

profile of v0, /device:TPU:0, one launch (start us, length us, event | category | flops | bytes accessed | tf_op | source)
XLA Modules:
  0.0 1710.5 jit_solution(1301464961985849624)
XLA Ops:
  24.7 33.2 %all_gather.116 = bf16[1024,256]{1,0:T(8,128)(2,1)S(1)} all-gather(bf16[128,256]{1,0:T(8,128)(2,1)S(1)} %copy-done.200), channel_id=1, replica_groups=mesh['row'=8,'col'=4] {'row'}, dimensions={0}, use_global_device_ids=true | all-gather | bytes 589824 | tf_op jit(solution)/shard_map/all_gather | solution.py:119
  59.1 31.5 %all_gather.117 = bf16[1024,256]{1,0:T(8,128)(2,1)S(1)} all-gather(bf16[128,256]{1,0:T(8,128)(2,1)S(1)} %copy-done.201), channel_id=1, replica_groups=mesh['row'=8,'col'=4] {'row'}, dimensions={0}, use_global_device_ids=true | all-gather | bytes 589824 | tf_op jit(solution)/shard_map/all_gather | solution.py:120
  90.7 33.4 %all_gather.115 = bf16[1024,256]{1,0:T(8,128)(2,1)} all-gather(bf16[128,256]{1,0:T(8,128)(2,1)S(1)} %copy-done.202), channel_id=1, replica_groups=mesh['row'=8,'col'=4] {'row'}, dimensions={0}, use_global_device_ids=true | all-gather | bytes 589824 | tf_op jit(solution)/shard_map/all_gather | solution.py:121
  226.6 40.7 %all-gather.38.cloned.1.call-done = bf16[1024,704]{0,1:T(8,128)(2,1)} async-done(((bf16[128,704]{0,1:T(8,128)(2,1)}), bf16[1024,704]{0,1:T(8,128)(2,1)}) %all-gather.38.cloned.1.call-update) | async-done | bytes 1441808 | tf_op jit(solution)/shard_map/all_gather | solution.py:123
  288.1 41.3 %all-gather.40.cloned.1.call-done = bf16[1024,704]{0,1:T(8,128)(2,1)} async-done(((bf16[128,704]{0,1:T(8,128)(2,1)}), bf16[1024,704]{0,1:T(8,128)(2,1)}) %all-gather.40.cloned.1.call-update) | async-done | bytes 1441808 | tf_op jit(solution)/shard_map/all_gather | solution.py:124
  333.1 39.4 %all-gather.42.cloned.1.call-done = bf16[704,1024]{1,0:T(8,128)(2,1)} async-done(((bf16[704,128]{1,0:T(8,128)(2,1)}), bf16[704,1024]{1,0:T(8,128)(2,1)}) %all-gather.42.cloned.1.call-update) | async-done | bytes 1441808 | tf_op jit(solution)/shard_map/all_gather | solution.py:125
  522.4 32.3 %reduce-scatter.40.cloned.1.call-done = f32[128,1024]{1,0:T(8,128)} async-done(((f32[512,1024]{1,0:T(8,128)}), f32[128,1024]{1,0:T(8,128)}) %reduce-scatter.40.cloned.1.call-update) | async-done | bytes 524304 | tf_op jit(solution)/shard_map/reduce_scatter | solution.py:71
  557.3 30.9 %reduce-scatter.44.cloned.1.call-done = f32[128,1024]{1,0:T(8,128)} async-done(((f32[512,1024]{1,0:T(8,128)}), f32[128,1024]{1,0:T(8,128)}) %reduce-scatter.44.cloned.1.call-update) | async-done | bytes 524304 | tf_op jit(solution)/shard_map/reduce_scatter | solution.py:71
  590.7 31.3 %reduce-scatter.50.cloned.1.call-done = f32[128,1024]{1,0:T(8,128)} async-done(((f32[512,1024]{1,0:T(8,128)}), f32[128,1024]{1,0:T(8,128)}) %reduce-scatter.50.cloned.1.call-update) | async-done | bytes 524304 | tf_op jit(solution)/shard_map/reduce_scatter | solution.py:71
  625.2 30.4 %reduce-scatter.34.cloned.1.call-done = f32[128,1024]{1,0:T(8,128)} async-done(((f32[512,1024]{1,0:T(8,128)}), f32[128,1024]{1,0:T(8,128)}) %reduce-scatter.34.cloned.1.call-update) | async-done | bytes 524304 | tf_op jit(solution)/shard_map/reduce_scatter | solution.py:71
  686.1 31.3 %reduce-scatter.52.cloned.1.call-done = f32[128,1024]{1,0:T(8,128)} async-done(((f32[512,1024]{1,0:T(8,128)}), f32[128,1024]{1,0:T(8,128)}) %reduce-scatter.52.cloned.1.call-update) | async-done | bytes 524304 | tf_op jit(solution)/shard_map/reduce_scatter | solution.py:71
  813.2 30.4 %reduce-scatter.38.cloned.1.call-done = f32[128,1024]{1,0:T(8,128)} async-done(((f32[512,1024]{1,0:T(8,128)}), f32[128,1024]{1,0:T(8,128)}) %reduce-scatter.38.cloned.1.call-update) | async-done | bytes 524304 | tf_op jit(solution)/shard_map/reduce_scatter | solution.py:71
  843.5 33.7 %reduce-scatter.60.cloned.1.call-done = f32[128,1024]{1,0:T(8,128)} async-done(((f32[512,1024]{1,0:T(8,128)}), f32[128,1024]{1,0:T(8,128)}) %reduce-scatter.60.cloned.1.call-update) | async-done | bytes 524304 | tf_op jit(solution)/shard_map/reduce_scatter | solution.py:71
  877.3 33.7 %reduce-scatter.56.cloned.1.call-done = f32[128,1024]{1,0:T(8,128)} async-done(((f32[512,1024]{1,0:T(8,128)}), f32[128,1024]{1,0:T(8,128)}) %reduce-scatter.56.cloned.1.call-update) | async-done | bytes 524304 | tf_op jit(solution)/shard_map/reduce_scatter | solution.py:71
  1020.5 34.3 %reduce-scatter.62.cloned.1.call-done = f32[128,1024]{1,0:T(8,128)} async-done(((f32[512,1024]{1,0:T(8,128)}), f32[128,1024]{1,0:T(8,128)}) %reduce-scatter.62.cloned.1.call-update) | async-done | bytes 524304 | tf_op jit(solution)/shard_map/reduce_scatter | solution.py:71
  1057.9 30.7 %reduce-scatter.46.cloned.1.call-done = f32[128,1024]{1,0:T(8,128)} async-done(((f32[512,1024]{1,0:T(8,128)}), f32[128,1024]{1,0:T(8,128)}) %reduce-scatter.46.cloned.1.call-update) | async-done | bytes 524304 | tf_op jit(solution)/shard_map/reduce_scatter | solution.py:71
  1129.5 65.5 %reduce-scatter.72.cloned.1.call-done = bf16[128,704]{1,0:T(8,128)(2,1)} async-done(((bf16[1024,704]{1,0:T(8,128)(2,1)}), bf16[128,704]{1,0:T(8,128)(2,1)}) %reduce-scatter.72.cloned.1.call-update) | async-done | bytes 180240
  1196.9 65.9 %reduce-scatter.74.cloned.1.call-done = bf16[128,704]{1,0:T(8,128)(2,1)} async-done(((bf16[1024,704]{1,0:T(8,128)(2,1)}), bf16[128,704]{1,0:T(8,128)(2,1)}) %reduce-scatter.74.cloned.1.call-update) | async-done | bytes 180240
  1264.6 65.9 %reduce-scatter.76.cloned.1.call-done = bf16[128,704]{1,0:T(8,128)(2,1)} async-done(((bf16[1024,704]{1,0:T(8,128)(2,1)}), bf16[128,704]{1,0:T(8,128)(2,1)}) %reduce-scatter.76.cloned.1.call-update) | async-done | bytes 180240
  1370.1 61.7 %reduce-scatter.70.cloned.1.call-done = bf16[128,256]{1,0:T(8,128)(2,1)} async-done(((bf16[1024,256]{1,0:T(8,128)(2,1)}), bf16[128,256]{1,0:T(8,128)(2,1)}) %reduce-scatter.70.cloned.1.call-update) | async-done | bytes 65552
  1433.5 63.4 %reduce-scatter.64.cloned.1.call-done = bf16[128,256]{1,0:T(8,128)(2,1)} async-done(((bf16[1024,256]{1,0:T(8,128)(2,1)}), bf16[128,256]{1,0:T(8,128)(2,1)}) %reduce-scatter.64.cloned.1.call-update) | async-done | bytes 65552 | tf_op jit(solution)/shard_map/reduce_scatter | solution.py:292
  1498.3 63.3 %reduce-scatter.66.cloned.1.call-done = bf16[128,256]{1,0:T(8,128)(2,1)} async-done(((bf16[1024,256]{1,0:T(8,128)(2,1)}), bf16[128,256]{1,0:T(8,128)(2,1)}) %reduce-scatter.66.cloned.1.call-update) | async-done | bytes 65552 | tf_op jit(solution)/shard_map/reduce_scatter | solution.py:295
  1563.1 63.3 %reduce-scatter.68.cloned.1.call-done = bf16[128,256]{1,0:T(8,128)(2,1)} async-done(((bf16[1024,256]{1,0:T(8,128)(2,1)}), bf16[128,256]{1,0:T(8,128)(2,1)}) %reduce-scatter.68.cloned.1.call-update) | async-done | bytes 65552 | tf_op jit(solution)/shard_map/reduce_scatter | solution.py:298
  1628.0 40.0 %all-reduce = (f32[1024]{0:T(1024)}, f32[1024]{0:T(1024)}) all-reduce(f32[1024]{0:T(1024)S(1)} %add_add_fusion.5, f32[1024]{0:T(1024)S(1)} %add_add_fusion.4), channel_id=1, replica_groups=mesh['row'=8,'col'=4] {'row','col'}, use_global_device_ids=true, to_apply=%region_64.69 | all-reduce | flops 2048 | bytes 16384 | tf_op jit(solution)/shard_map/psum | solution.py:314
  (976 shorter events, 664.5 us)
Async XLA Ops:
  7.2 150.8 %all-gather.74.cloned.1.call-start = ((), (), s32[]{:S(2)}) async-start(), calls=%async_computation.61 | async-start | bytes 1310720 | tf_op jit(solution)/shard_map/all_gather | solution.py:133
  9.5 153.6 %all-gather.76.cloned.1.call-start = ((), (), s32[]{:S(2)}) async-start(), calls=%async_computation.62 | async-start | bytes 1310720 | tf_op jit(solution)/shard_map/all_gather | solution.py:133
  10.3 158.0 %all-gather.78.cloned.1.call-start = ((), (), s32[]{:S(2)}) async-start(), calls=%async_computation.63 | async-start | bytes 1310720 | tf_op jit(solution)/shard_map/all_gather | solution.py:133
  11.0 163.1 %all-gather.80.cloned.1.call-start = ((), (), s32[]{:S(2)}) async-start(), calls=%async_computation.64 | async-start | bytes 1310720 | tf_op jit(solution)/shard_map/all_gather | solution.py:133
  11.6 180.9 %all-gather.82.cloned.1.call-start = ((), (), s32[]{:S(2)}) async-start(), calls=%async_computation.65 | async-start | bytes 1310720 | tf_op jit(solution)/shard_map/all_gather | solution.py:134
  12.7 209.6 %reduce-scatter.32.cloned.1.call-start = ((), (), s32[]{:S(2)}) async-start(), calls=%async_computation.23 | async-start | bytes 2621440 | tf_op jit(solution)/shard_map/reduce_scatter | solution.py:71
  226.5 184.8 %reduce-scatter.48.cloned.1.call-start = ((), (), s32[]{:S(2)}) async-start(), calls=%async_computation.42 | async-start | bytes 2621440 | tf_op jit(solution)/shard_map/reduce_scatter | solution.py:71
  457.7 164.3 %reduce-scatter.50.cloned.1.call-start = ((), (), s32[]{:S(2)}) async-start(), calls=%async_computation.44 | async-start | bytes 2621440 | tf_op jit(solution)/shard_map/reduce_scatter | solution.py:71
  472.0 183.6 %reduce-scatter.34.cloned.1.call-start = ((), (), s32[]{:S(2)}) async-start(), calls=%async_computation.28 | async-start | bytes 2621440 | tf_op jit(solution)/shard_map/reduce_scatter | solution.py:71
  476.9 198.8 %all-gather.46.cloned.1.call-start = ((), (), s32[]{:S(2)}) async-start(), calls=%async_computation.31 | async-start | bytes 1310720 | tf_op jit(solution)/shard_map/all_gather | solution.py:67
  972.2 153.9 %all-gather.44.cloned.1.call-start = ((), (), s32[]{:S(2)}) async-start(), calls=%async_computation.29 | async-start | bytes 1310720 | tf_op jit(solution)/shard_map/all_gather | solution.py:279
  972.8 222.3 %reduce-scatter.72.cloned.1.call-start = ((), (), s32[]{:S(2)}) async-start(), calls=%async_computation.70 | async-start | bytes 1769472
  979.7 283.1 %reduce-scatter.74.cloned.1.call-start = ((), (), s32[]{:S(2)}) async-start(), calls=%async_computation.71 | async-start | bytes 1769472
  987.3 343.3 %reduce-scatter.76.cloned.1.call-start = ((), (), s32[]{:S(2)}) async-start(), calls=%async_computation.72 | async-start | bytes 1769472
  994.2 353.5 %all-gather.64.cloned.1.call-start = ((), (), s32[]{:S(2)}) async-start(), calls=%async_computation.49 | async-start | bytes 1310720 | tf_op jit(solution)/shard_map/all_gather | solution.py:282
  995.0 371.0 %all-gather.48.cloned.1.call-start = ((), (), s32[]{:S(2)}) async-start(), calls=%async_computation.33 | async-start | bytes 1310720 | tf_op jit(solution)/shard_map/all_gather | solution.py:279
  995.7 436.1 %reduce-scatter.70.cloned.1.call-start = ((), (), s32[]{:S(2)}) async-start(), calls=%async_computation.69 | async-start | bytes 589824
  1000.7 496.1 %reduce-scatter.64.cloned.1.call-start = ((), (), s32[]{:S(2)}) async-start(), calls=%async_computation.58 | async-start | bytes 589824 | tf_op jit(solution)/shard_map/reduce_scatter | solution.py:292
  1005.1 556.5 %reduce-scatter.66.cloned.1.call-start = ((), (), s32[]{:S(2)}) async-start(), calls=%async_computation.59 | async-start | bytes 589824 | tf_op jit(solution)/shard_map/reduce_scatter | solution.py:295
  1009.7 616.8 %reduce-scatter.68.cloned.1.call-start = ((), (), s32[]{:S(2)}) async-start(), calls=%async_computation.60 | async-start | bytes 589824 | tf_op jit(solution)/shard_map/reduce_scatter | solution.py:298
  1015.1 652.9 %all-gather.72.cloned.1.call-start = ((), (), s32[]{:S(2)}) async-start(), calls=%async_computation.57 | async-start | bytes 1310720 | tf_op jit(solution)/shard_map/all_gather | solution.py:282
  1091.0 579.3 %all-gather.68.cloned.1.call-start = ((), (), s32[]{:S(2)}) async-start(), calls=%async_computation.53 | async-start | bytes 1310720 | tf_op jit(solution)/shard_map/all_gather | solution.py:282
  1091.6 588.6 %all-gather.56.cloned.1.call-start = ((), (), s32[]{:S(2)}) async-start(), calls=%async_computation.41 | async-start | bytes 1310720 | tf_op jit(solution)/shard_map/all_gather | solution.py:279
  1092.1 606.3 %all-gather.52.cloned.1.call-start = ((), (), s32[]{:S(2)}) async-start(), calls=%async_computation.37 | async-start | bytes 1310720 | tf_op jit(solution)/shard_map/all_gather | solution.py:279
  (291 other events, 6778.1 us)
Sparse Core Ops, SparseCore 0:
  224.3 42.9 all-gather.37
  286.4 42.9 all-gather.39
  331.3 41.1 all-gather.41
  489.3 31.1 reduce-scatter.35
  523.5 31.1 reduce-scatter.39
  557.1 31.1 reduce-scatter.43
  590.8 31.1 reduce-scatter.49
  624.4 31.1 reduce-scatter.33
  686.1 31.1 reduce-scatter.51
  778.7 31.1 reduce-scatter.53
  812.3 31.1 reduce-scatter.37
  846.0 31.1 reduce-scatter.59
  879.8 31.1 reduce-scatter.55
  955.7 31.1 reduce-scatter.57
  989.3 31.1 reduce-scatter.41
  1023.6 31.1 reduce-scatter.61
  1057.4 31.1 reduce-scatter.45
  1129.4 65.5 reduce-scatter.71
  1198.3 64.4 reduce-scatter.73
  1266.2 64.3 reduce-scatter.75
  1369.2 62.6 reduce-scatter.69
  1435.2 61.6 reduce-scatter.63
  1500.0 61.5 reduce-scatter.65
  1564.8 61.5 reduce-scatter.67
  (26 shorter events, 458.0 us)
where the time goes:
time: 1720 us; the launch traced here: 1710 us
  waiting for transfers between devices  1140 us (66%)
  blocking collectives  166 us (10%)
  matrix products  148 us (9%)
  local copies, waits for them, and re-layouts  131 us (8%)
  other arithmetic  99.4 us (6%)
  between operations  18.5 us (1%)
    reduce_scatter x16, waiting for transfers between devices, reduce_tokens(): return lax.psum_scatter(values, 'col', scatter_dimension=0, tiled=True)  417 us
    unnamed x54, waiting for transfers between devices  270 us
    all_gather x8, waiting for transfers between devices, spread_tokens(): return lax.all_gather(values, 'col', axis=0, tiled=True)  72.8 us
    reduce_scatter x1, waiting for transfers between devices, body(): lax.psum_scatter(grads_full[0].astype(jnp.bfloat16), 'row', scatter_dimen...  63.4 us
    reduce_scatter x1, waiting for transfers between devices, body(): lax.psum_scatter(grads_full[1].astype(jnp.bfloat16), 'row', scatter_dimen...  63.3 us
    reduce_scatter x1, waiting for transfers between devices, body(): lax.psum_scatter(grads_full[2].astype(jnp.bfloat16), 'row', scatter_dimen...  63.3 us
    all_gather x4, waiting for transfers between devices, body(): lax.all_gather(packed_out.astype(jnp.float32).astype(jnp.bfloat16), 'col'...  55.5 us
    dot_general x28, matrix products, product(): return jnp.dot(left, right, preferred_element_type=jnp.float32)  46.7 us
  transfers between devices with their start and end apart: 50, of which 37 were waited for; matrix products, arithmetic and copies ran while one was open for 18% of the time, Pallas kernels for 0%

commit v1 on v0

--- a/solution.py
+++ b/solution.py
@@ -1,3 +1,4 @@
+import functools
 import jax
 import jax.numpy as jnp
 from jax import lax
@@ -9,6 +10,30 @@
 MICRO = 4
 EPSILON = 1e-06
 MASKED = -1e30
+
+
+def _deliver_screen(s0, comm_axis, on_dim):
+    spare, kept_arr, t1 = (lax.axis_size(comm_axis), lax.axis_index(comm_axis), s0.shape[on_dim])
+    pile = tuple(((dev_i, (dev_i + 1) % spare) for dev_i in range(spare)))
+    entries = tuple(((dev_i, (dev_i - 1) % spare) for dev_i in range(spare)))
+    item_now = jnp.zeros((*s0.shape[:on_dim], spare * t1, *s0.shape[on_dim + 1 :]), s0.dtype)
+    item_now = lax.dynamic_update_slice_in_dim(item_now, s0, kept_arr * t1, axis=on_dim)
+    met_up = step_out = s0
+    part_now = spare // 2
+    for k in range(1, part_now + 1):
+        met_up = lax.ppermute(met_up, comm_axis, pile)
+        item_now = lax.dynamic_update_slice_in_dim(
+            item_now, met_up, (kept_arr - k) % spare * t1, axis=on_dim
+        )
+        if k < spare - part_now:
+            step_out = lax.ppermute(step_out, comm_axis, entries)
+            item_now = lax.dynamic_update_slice_in_dim(
+                item_now, step_out, (kept_arr + k) % spare * t1, axis=on_dim
+            )
+    return item_now
+
+
+build_views = functools.partial(_deliver_screen, comm_axis="col", on_dim=0)
 
 
 def product(left, right):
@@ -64,7 +89,7 @@
 
 
 def spread_tokens(values):
-    return lax.all_gather(values, "col", axis=0, tiled=True)
+    return build_views(values)
 
 
 def reduce_tokens(values):

time: 1720 us -> 1560 us (0.907)
  waiting for transfers between devices: 1140 us -> 964 us
  local copies, waits for them, and re-layouts: 131 us -> 151 us
    reduce_scatter x16, waiting for transfers between devices: 417 us -> 253 us  [reduce_tokens(): return lax.psum_scatter(values, 'col', scatter_dimension=0, tiled=True)]
    all_gather x8 -> x0, waiting for transfers between devices: 72.8 us -> none  [spread_tokens(): return lax.all_gather(values, 'col', axis=0, tiled=True)]
    ppermute x0 -> x24, waiting for transfers between devices: none -> 62.7 us  [the longest x16 62.4 us: _deliver_screen(): met_up = lax.ppermute(met_up, comm_axis, pile)]
    unnamed x54 -> x46, waiting for transfers between devices: 270 us -> 256 us
    unnamed x543 -> x579, local copies, waits for them, and re-layouts: 43.7 us -> 49 us
  transfers between devices with their start and end apart: 50 -> 66, of which waited for: 37 -> 43; matrix products, arithmetic and copies ran while one was open for 18% -> 22% of each run, Pallas kernels for 0% -> 0%
where the time goes in v1:
time: 1560 us; the launch traced here: 1550 us
  waiting for transfers between devices  964 us (62%)
  blocking collectives  167 us (11%)
  local copies, waits for them, and re-layouts  151 us (10%)
  matrix products  138 us (9%)
  other arithmetic  92.4 us (6%)
  between operations  18.8 us (1%)
  starting transfers between devices  18.5 us (1%)
    unnamed x46, waiting for transfers between devices  256 us
    reduce_scatter x16, waiting for transfers between devices, reduce_tokens(): return lax.psum_scatter(values, 'col', scatter_dimension=0, tiled=True)  253 us
    reduce_scatter x1, waiting for transfers between devices, body(): lax.psum_scatter(grads_full[0].astype(jnp.bfloat16), 'row', scatter_dimen...  63.6 us
    reduce_scatter x1, waiting for transfers between devices, body(): lax.psum_scatter(grads_full[1].astype(jnp.bfloat16), 'row', scatter_dimen...  63.5 us
    reduce_scatter x1, waiting for transfers between devices, body(): lax.psum_scatter(grads_full[2].astype(jnp.bfloat16), 'row', scatter_dimen...  63.4 us
    all_gather x4, waiting for transfers between devices, body(): lax.all_gather(packed_out.astype(jnp.float32).astype(jnp.bfloat16), 'col'...  63.2 us
    ppermute x16, waiting for transfers between devices, _deliver_screen(): met_up = lax.ppermute(met_up, comm_axis, pile)  62.4 us
    unnamed x579, local copies, waits for them, and re-layouts  49 us
  transfers between devices with their start and end apart: 66, of which 43 were waited for; matrix products, arithmetic and copies ran while one was open for 22% of the time, Pallas kernels for 0%

profile of v1, /device:TPU:0, one launch (start us, length us, event | category | flops | bytes accessed | tf_op | source)
XLA Modules:
  0.0 1550.2 jit_solution(268541260761328087)
XLA Ops:
  24.2 33.2 %all_gather.92 = bf16[1024,256]{1,0:T(8,128)(2,1)S(1)} all-gather(bf16[128,256]{1,0:T(8,128)(2,1)S(1)} %copy-done.211), channel_id=1, replica_groups=mesh['row'=8,'col'=4] {'row'}, dimensions={0}, use_global_device_ids=true | all-gather | bytes 589824 | tf_op jit(solution)/shard_map/all_gather | solution.py:144
  58.6 31.5 %all_gather.93 = bf16[1024,256]{1,0:T(8,128)(2,1)S(1)} all-gather(bf16[128,256]{1,0:T(8,128)(2,1)S(1)} %copy-done.212), channel_id=1, replica_groups=mesh['row'=8,'col'=4] {'row'}, dimensions={0}, use_global_device_ids=true | all-gather | bytes 589824 | tf_op jit(solution)/shard_map/all_gather | solution.py:145
  90.2 33.4 %all_gather.91 = bf16[1024,256]{1,0:T(8,128)(2,1)} all-gather(bf16[128,256]{1,0:T(8,128)(2,1)S(1)} %copy-done.213), channel_id=1, replica_groups=mesh['row'=8,'col'=4] {'row'}, dimensions={0}, use_global_device_ids=true | all-gather | bytes 589824 | tf_op jit(solution)/shard_map/all_gather | solution.py:146
  124.5 28.3 %all_gather.94 = bf16[256,1024]{1,0:T(8,128)(2,1)} all-gather(bf16[256,128]{1,0:T(8,128)(2,1)S(1)} %copy-done.214), channel_id=1, replica_groups=mesh['row'=8,'col'=4] {'row'}, dimensions={1}, use_global_device_ids=true | all-gather | bytes 589824 | tf_op jit(solution)/shard_map/all_gather | solution.py:147
  232.0 34.5 %all-gather.32.cloned.1.call-done = bf16[704,1024]{1,0:T(8,128)(2,1)} async-done(((bf16[704,128]{1,0:T(8,128)(2,1)}), bf16[704,1024]{1,0:T(8,128)(2,1)}) %all-gather.32.cloned.1.call-update) | async-done | bytes 1441808 | tf_op jit(solution)/shard_map/all_gather | solution.py:150
  273.2 36.6 %all-gather.30.cloned.1.call-done = bf16[1024,704]{0,1:T(8,128)(2,1)} async-done(((bf16[128,704]{0,1:T(8,128)(2,1)}), bf16[1024,704]{0,1:T(8,128)(2,1)}) %all-gather.30.cloned.1.call-update) | async-done | bytes 1441808 | tf_op jit(solution)/shard_map/all_gather | solution.py:149
  313.1 39.8 %all-gather.28.cloned.1.call-done = bf16[1024,704]{0,1:T(8,128)(2,1)} async-done(((bf16[128,704]{0,1:T(8,128)(2,1)}), bf16[1024,704]{0,1:T(8,128)(2,1)}) %all-gather.28.cloned.1.call-update) | async-done | bytes 1441808 | tf_op jit(solution)/shard_map/all_gather | solution.py:148
  377.4 25.6 %reduce-scatter.36.cloned.1.call-done = f32[128,1024]{1,0:T(8,128)} async-done(((f32[512,1024]{1,0:T(8,128)}), f32[128,1024]{1,0:T(8,128)}) %reduce-scatter.36.cloned.1.call-update) | async-done | bytes 524304 | tf_op jit(solution)/shard_map/reduce_scatter | solution.py:96
  453.6 17.4 %reduce-scatter.52.cloned.1.call-done = f32[128,1024]{1,0:T(8,128)} async-done(((f32[512,1024]{1,0:T(8,128)}), f32[128,1024]{1,0:T(8,128)}) %reduce-scatter.52.cloned.1.call-update) | async-done | bytes 524304 | tf_op jit(solution)/shard_map/reduce_scatter | solution.py:96
  613.2 33.7 %reduce-scatter.54.cloned.1.call-done = f32[128,1024]{1,0:T(8,128)} async-done(((f32[512,1024]{1,0:T(8,128)}), f32[128,1024]{1,0:T(8,128)}) %reduce-scatter.54.cloned.1.call-update) | async-done | bytes 524304 | tf_op jit(solution)/shard_map/reduce_scatter | solution.py:96
  650.6 29.9 %reduce-scatter.34.cloned.1.call-done = f32[128,1024]{1,0:T(8,128)} async-done(((f32[512,1024]{1,0:T(8,128)}), f32[128,1024]{1,0:T(8,128)}) %reduce-scatter.34.cloned.1.call-update) | async-done | bytes 524304 | tf_op jit(solution)/shard_map/reduce_scatter | solution.py:96
  680.4 34.3 %reduce-scatter.60.cloned.1.call-done = f32[128,1024]{1,0:T(8,128)} async-done(((f32[512,1024]{1,0:T(8,128)}), f32[128,1024]{1,0:T(8,128)}) %reduce-scatter.60.cloned.1.call-update) | async-done | bytes 524304 | tf_op jit(solution)/shard_map/reduce_scatter | solution.py:96
  714.7 33.7 %reduce-scatter.56.cloned.1.call-done = f32[128,1024]{1,0:T(8,128)} async-done(((f32[512,1024]{1,0:T(8,128)}), f32[128,1024]{1,0:T(8,128)}) %reduce-scatter.56.cloned.1.call-update) | async-done | bytes 524304 | tf_op jit(solution)/shard_map/reduce_scatter | solution.py:96
  864.6 30.1 %reduce-scatter.46.cloned.1.call-done = f32[128,1024]{1,0:T(8,128)} async-done(((f32[512,1024]{1,0:T(8,128)}), f32[128,1024]{1,0:T(8,128)}) %reduce-scatter.46.cloned.1.call-update) | async-done | bytes 524304 | tf_op jit(solution)/shard_map/reduce_scatter | solution.py:96
  897.3 30.9 %reduce-scatter.42.cloned.1.call-done = f32[128,1024]{1,0:T(8,128)} async-done(((f32[512,1024]{1,0:T(8,128)}), f32[128,1024]{1,0:T(8,128)}) %reduce-scatter.42.cloned.1.call-update) | async-done | bytes 524304 | tf_op jit(solution)/shard_map/reduce_scatter | solution.py:96
  932.8 64.5 %reduce-scatter.72.cloned.1.call-done = bf16[128,704]{1,0:T(8,128)(2,1)} async-done(((bf16[1024,704]{1,0:T(8,128)(2,1)}), bf16[128,704]{1,0:T(8,128)(2,1)}) %reduce-scatter.72.cloned.1.call-update) | async-done | bytes 180240
  999.1 66.0 %reduce-scatter.74.cloned.1.call-done = bf16[128,704]{1,0:T(8,128)(2,1)} async-done(((bf16[1024,704]{1,0:T(8,128)(2,1)}), bf16[128,704]{1,0:T(8,128)(2,1)}) %reduce-scatter.74.cloned.1.call-update) | async-done | bytes 180240
  1067.0 66.0 %reduce-scatter.76.cloned.1.call-done = bf16[128,704]{1,0:T(8,128)(2,1)} async-done(((bf16[1024,704]{1,0:T(8,128)(2,1)}), bf16[128,704]{1,0:T(8,128)(2,1)}) %reduce-scatter.76.cloned.1.call-update) | async-done | bytes 180240
  1147.2 50.8 %reduce-scatter.70.cloned.1.call-done = bf16[128,256]{1,0:T(8,128)(2,1)} async-done(((bf16[1024,256]{1,0:T(8,128)(2,1)}), bf16[128,256]{1,0:T(8,128)(2,1)}) %reduce-scatter.70.cloned.1.call-update) | async-done | bytes 65552
  1235.9 63.6 %reduce-scatter.64.cloned.1.call-done = bf16[128,256]{1,0:T(8,128)(2,1)} async-done(((bf16[1024,256]{1,0:T(8,128)(2,1)}), bf16[128,256]{1,0:T(8,128)(2,1)}) %reduce-scatter.64.cloned.1.call-update) | async-done | bytes 65552 | tf_op jit(solution)/shard_map/reduce_scatter | solution.py:317
  1301.0 63.5 %reduce-scatter.66.cloned.1.call-done = bf16[128,256]{1,0:T(8,128)(2,1)} async-done(((bf16[1024,256]{1,0:T(8,128)(2,1)}), bf16[128,256]{1,0:T(8,128)(2,1)}) %reduce-scatter.66.cloned.1.call-update) | async-done | bytes 65552 | tf_op jit(solution)/shard_map/reduce_scatter | solution.py:320
  1365.9 63.4 %reduce-scatter.68.cloned.1.call-done = bf16[128,256]{1,0:T(8,128)(2,1)} async-done(((bf16[1024,256]{1,0:T(8,128)(2,1)}), bf16[128,256]{1,0:T(8,128)(2,1)}) %reduce-scatter.68.cloned.1.call-update) | async-done | bytes 65552 | tf_op jit(solution)/shard_map/reduce_scatter | solution.py:323
  1431.9 40.5 %all-reduce = (f32[1024]{0:T(1024)}, f32[1024]{0:T(1024)}) all-reduce(f32[1024]{0:T(1024)S(1)} %add_add_fusion.5, f32[1024]{0:T(1024)S(1)} %add_add_fusion.4), channel_id=1, replica_groups=mesh['row'=8,'col'=4] {'row','col'}, use_global_device_ids=true, to_apply=%region_64.69 | all-reduce | flops 2048 | bytes 16384 | tf_op jit(solution)/shard_map/psum | solution.py:339
  1485.5 16.0 %all-gather.40.cloned.1.call-done = bf16[512,1024]{1,0:T(8,128)(2,1)} async-done(((bf16[128,1024]{1,0:T(8,128)(2,1)}), bf16[512,1024]{1,0:T(8,128)(2,1)}) %all-gather.40.cloned.1.call-update) | async-done | bytes 1048592 | tf_op jit(solution)/shard_map/all_gather | solution.py:304
  (1070 shorter events, 564.1 us)
Async XLA Ops:
  11.0 161.9 %all-gather.56.cloned.1.call-start = ((), (), s32[]{:S(2)}) async-start(), calls=%async_computation.56 | async-start | bytes 1310720 | tf_op jit(solution)/shard_map/all_gather | solution.py:158
  11.6 196.9 %all-gather.58.cloned.1.call-start = ((), (), s32[]{:S(2)}) async-start(), calls=%async_computation.57 | async-start | bytes 1310720 | tf_op jit(solution)/shard_map/all_gather | solution.py:159
  12.6 208.8 %reduce-scatter.32.cloned.1.call-start = ((), (), s32[]{:S(2)}) async-start(), calls=%async_computation.23 | async-start | bytes 2621440 | tf_op jit(solution)/shard_map/reduce_scatter | solution.py:96
  193.0 176.3 %all-gather.60.cloned.1.call-start = ((), (), s32[]{:S(2)}) async-start(), calls=%async_computation.58 | async-start | bytes 1310720 | tf_op jit(solution)/shard_map/all_gather | solution.py:159
  193.5 209.5 %reduce-scatter.36.cloned.1.call-start = ((), (), s32[]{:S(2)}) async-start(), calls=%async_computation.29 | async-start | bytes 2621440 | tf_op jit(solution)/shard_map/reduce_scatter | solution.py:96
  208.4 245.2 %reduce-scatter.48.cloned.1.call-start = ((), (), s32[]{:S(2)}) async-start(), calls=%async_computation.38 | async-start | bytes 2621440 | tf_op jit(solution)/shard_map/reduce_scatter | solution.py:96
  532.7 182.0 %reduce-scatter.60.cloned.1.call-start = ((), (), s32[]{:S(2)}) async-start(), calls=%async_computation.47 | async-start | bytes 2621440 | tf_op jit(solution)/shard_map/reduce_scatter | solution.py:96
  566.2 182.2 %reduce-scatter.56.cloned.1.call-start = ((), (), s32[]{:S(2)}) async-start(), calls=%async_computation.44 | async-start | bytes 2621440 | tf_op jit(solution)/shard_map/reduce_scatter | solution.py:96
  602.9 257.5 %reduce-scatter.38.cloned.1.call-start = ((), (), s32[]{:S(2)}) async-start(), calls=%async_computation.30 | async-start | bytes 2621440 | tf_op jit(solution)/shard_map/reduce_scatter | solution.py:96
  812.1 185.2 %reduce-scatter.72.cloned.1.call-start = ((), (), s32[]{:S(2)}) async-start(), calls=%async_computation.62 | async-start | bytes 1769472
  822.6 242.6 %reduce-scatter.74.cloned.1.call-start = ((), (), s32[]{:S(2)}) async-start(), calls=%async_computation.63 | async-start | bytes 1769472
  830.2 302.9 %reduce-scatter.76.cloned.1.call-start = ((), (), s32[]{:S(2)}) async-start(), calls=%async_computation.64 | async-start | bytes 1769472
  837.9 360.1 %reduce-scatter.70.cloned.1.call-start = ((), (), s32[]{:S(2)}) async-start(), calls=%async_computation.61 | async-start | bytes 589824
  843.4 372.0 %all-gather.42.cloned.1.call-start = ((), (), s32[]{:S(2)}) async-start(), calls=%async_computation.40 | async-start | bytes 1310720 | tf_op jit(solution)/shard_map/all_gather | solution.py:307
  844.1 389.4 %all-gather.34.cloned.1.call-start = ((), (), s32[]{:S(2)}) async-start(), calls=%async_computation.28 | async-start | bytes 1310720 | tf_op jit(solution)/shard_map/all_gather | solution.py:304
  844.7 454.8 %reduce-scatter.64.cloned.1.call-start = ((), (), s32[]{:S(2)}) async-start(), calls=%async_computation.50 | async-start | bytes 589824 | tf_op jit(solution)/shard_map/reduce_scatter | solution.py:317
  849.4 515.1 %reduce-scatter.66.cloned.1.call-start = ((), (), s32[]{:S(2)}) async-start(), calls=%async_computation.51 | async-start | bytes 589824 | tf_op jit(solution)/shard_map/reduce_scatter | solution.py:320
  853.9 575.4 %reduce-scatter.68.cloned.1.call-start = ((), (), s32[]{:S(2)}) async-start(), calls=%async_computation.52 | async-start | bytes 589824 | tf_op jit(solution)/shard_map/reduce_scatter | solution.py:323
  859.6 612.8 %all-gather.48.cloned.1.call-start = ((), (), s32[]{:S(2)}) async-start(), calls=%async_computation.49 | async-start | bytes 1310720 | tf_op jit(solution)/shard_map/all_gather | solution.py:307
  897.2 577.5 %all-gather.46.cloned.1.call-start = ((), (), s32[]{:S(2)}) async-start(), calls=%async_computation.46 | async-start | bytes 1310720 | tf_op jit(solution)/shard_map/all_gather | solution.py:307
  930.6 552.6 %all-gather.44.cloned.1.call-start = ((), (), s32[]{:S(2)}) async-start(), calls=%async_computation.43 | async-start | bytes 1310720 | tf_op jit(solution)/shard_map/all_gather | solution.py:307
  931.2 570.3 %all-gather.40.cloned.1.call-start = ((), (), s32[]{:S(2)}) async-start(), calls=%async_computation.37 | async-start | bytes 1310720 | tf_op jit(solution)/shard_map/all_gather | solution.py:304
  932.0 587.9 %all-gather.38.cloned.1.call-start = ((), (), s32[]{:S(2)}) async-start(), calls=%async_computation.34 | async-start | bytes 1310720 | tf_op jit(solution)/shard_map/all_gather | solution.py:304
  932.7 605.4 %all-gather.36.cloned.1.call-start = ((), (), s32[]{:S(2)}) async-start(), calls=%async_computation.31 | async-start | bytes 1310720 | tf_op jit(solution)/shard_map/all_gather | solution.py:304
  (325 other events, 6757.1 us)
Sparse Core Ops, SparseCore 0:
  223.5 42.9 all-gather.31
  268.5 41.1 all-gather.29
  311.8 41.1 all-gather.27
  371.8 31.1 reduce-scatter.35
  406.0 31.1 reduce-scatter.47
  439.7 31.2 reduce-scatter.51
  548.4 31.1 reduce-scatter.39
  582.0 31.1 reduce-scatter.49
  615.7 31.1 reduce-scatter.53
  649.2 31.1 reduce-scatter.33
  683.5 31.1 reduce-scatter.59
  717.2 31.1 reduce-scatter.55
  757.9 35.1 reduce-scatter.37
  796.1 31.1 reduce-scatter.61
  829.8 31.1 reduce-scatter.57
  863.4 31.1 reduce-scatter.45
  897.0 31.1 reduce-scatter.41
  931.7 65.5 reduce-scatter.71
  1000.7 64.4 reduce-scatter.73
  1068.4 64.5 reduce-scatter.75
  1136.4 61.5 reduce-scatter.69
  1236.8 62.6 reduce-scatter.63
  1302.8 61.6 reduce-scatter.65
  1367.6 61.6 reduce-scatter.67
  (18 shorter events, 331.6 us)
